TPU v7x, 32 devices: a whole 2x2x4 slice. The times are simulated.
32 devices in a mesh: batch: 2 (over core), expert: 4 (over y, x), dim: 4 (over z).
Axes of the slice: x: 2, y: 2, z: 4, core: 2. Of those that a mesh axis runs over, the one named last changes fastest.
Arguments:
- inputs: bfloat16 [2048, 4096], P('batch', 'dim'), may hold values from -6 to 6
- expert_ids: int32 [2048, 4], P('batch'), may hold values from 0 to 7, all different within a row; in each aligned block of 1024 rows (0 to 1023, 1024 to 2047, ...) at most 1024 rows name the same one
- gate_weight: bfloat16 [4096, 8], P('dim'), may hold values from -0.09375 to 0.09375
- reduce_weight: bfloat16 [8, 4096, 256], P('expert', ('dim', 'batch')), may hold values from -0.09375 to 0.09375
- middle_weight: bfloat16 [8, 256, 256], P('expert', 'batch'), may hold values from -0.375 to 0.375
- expand_weight: bfloat16 [8, 4096, 256], P('expert', ('dim', 'batch')), may hold values from -0.375 to 0.375
- bias: float32 [4096], P('dim'), may hold values from -3 to 3
Outputs:
- crossed: bfloat16 [2048, 4096], P(('batch', 'expert'), 'dim')
Inputs may be any that keep to these rules, and one draw needn't show every extreme that they name: `expert_ids`: each row names 4 different experts; in each aligned block of 1024 rows (the examples of one index of batch) no expert is named by more than 1024 rows, and in some block one expert is named by exactly 1024 rows.
All inputs are finite; a program needn't handle non-finite values.
Results may differ from a plain program's by a relative error of at most 0.012.
Values may be sent and summed in bfloat16 or wider, within the bound.
No kernel may reach another device: no remote copies, remote signals or barrier semaphores. Data moves between devices by JAX's collectives and lax.ppermute only.
A program may use at most 64 MiB of HBM per device.

v0:
```python
import jax
import jax.numpy as jnp
from jax import lax
from jax.sharding import PartitionSpec as P

CAP = 1024


def pick_rows(expert_rows, slot_pick):
    return expert_rows[slot_pick]


def on_device(inputs, expert_ids, gate_weight, reduce_weight, middle_weight, expand_weight, bias):
    tok_count, feature_width = inputs.shape
    local_count = reduce_weight.shape[0]
    all_experts = gate_weight.shape[1]
    first_expert = lax.axis_index("expert") * local_count
    numbers = jnp.arange(all_experts, dtype=jnp.int32)
    chosen = jnp.sum((expert_ids[:, :, None] == numbers[None, None, :]).astype(jnp.int32), axis=1)
    position = jnp.cumsum(chosen, axis=0) - chosen
    chosen_here = lax.dynamic_slice_in_dim(chosen, first_expert, local_count, 1)
    position_here = lax.dynamic_slice_in_dim(position, first_expert, local_count, 1)
    target = jnp.where(chosen_here > 0, position_here, CAP).T
    expert_grid = jnp.broadcast_to(
        jnp.arange(local_count, dtype=jnp.int32)[:, None], (local_count, tok_count)
    )
    token_grid = jnp.broadcast_to(
        jnp.arange(tok_count, dtype=jnp.int32)[None, :], (local_count, tok_count)
    )
    slot_owner = (
        jnp.full((local_count, CAP), tok_count, jnp.int32)
        .at[expert_grid, target]
        .set(token_grid, mode="drop")
    )
    padded = jnp.concatenate([inputs, jnp.zeros((1, feature_width), inputs.dtype)], axis=0)
    dispatched = padded[slot_owner]
    logits_part = jnp.dot(inputs, gate_weight, preferred_element_type=jnp.float32)
    projected = jnp.einsum(
        "esd,edr->esr",
        dispatched,
        lax.all_gather(reduce_weight, "batch", axis=1, tiled=True),
        preferred_element_type=jnp.float32,
    )
    middle_full = lax.all_gather(middle_weight, "batch", axis=1, tiled=True)
    logits, summed = (
        lax.psum(logits_part.astype(jnp.bfloat16), "dim").astype(jnp.float32),
        lax.psum(projected.astype(jnp.bfloat16), "dim").astype(jnp.float32),
    )
    squashed = jnp.tanh(summed).astype(jnp.bfloat16)
    inner_mix = jnp.einsum(
        "esj,eij->esi", squashed, middle_full, preferred_element_type=jnp.float32
    )
    hidden = jnp.tanh(inner_mix).astype(jnp.bfloat16)
    expanded = jnp.einsum(
        "esr,edr->esd",
        hidden,
        lax.all_gather(expand_weight, "batch", axis=1, tiled=True),
        preferred_element_type=jnp.float32,
    )
    gate_values = jax.nn.sigmoid(
        lax.dynamic_slice_in_dim(logits, first_expert, local_count, 1)
    ) * chosen_here.astype(jnp.float32)
    slot_read = jnp.minimum(position_here, CAP - 1).T
    picked = jax.vmap(pick_rows)(expanded, slot_read)
    expert_mix = jnp.sum(gate_values.T[:, :, None] * (picked + bias[None, None, :]), axis=0)
    partial_term = inputs.astype(jnp.float32) * expert_mix
    summed_rows = lax.psum_scatter(
        partial_term.astype(jnp.bfloat16), "expert", scatter_dimension=0, tiled=True
    ).astype(jnp.float32)
    row_count = summed_rows.shape[0]
    own_rows = lax.dynamic_slice_in_dim(inputs, lax.axis_index("expert") * row_count, row_count, 0)
    return (own_rows.astype(jnp.float32) + summed_rows).astype(jnp.bfloat16)


def solution(mesh):
    in_specs = (
        P("batch", "dim"),
        P("batch", None),
        P("dim", None),
        P("expert", ("dim", "batch"), None),
        P("expert", "batch", None),
        P("expert", ("dim", "batch"), None),
        P("dim"),
    )
    out_specs = P(("batch", "expert"), "dim")
    return jax.shard_map(
        on_device, mesh=mesh, in_specs=in_specs, out_specs=out_specs, check_vma=False
    )
```

profile of v0, /device:TPU:0, one launch (start us, length us, event | category | flops | bytes accessed | tf_op | source)
XLA Modules:
  0.0 194.0 jit_solution(1393359733203876569)
XLA Ops:
  6.5 0.7 all-gather.3.cloned.1.call-update
  7.3 0.7 all-gather.5.cloned.1.call-update
  8.1 0.7 convert_reduce_fusion
  8.8 2.3 %reduce-window.6 = s32[8,8,128]{2,1,0:T(8,128)S(1)} reduce-window(s32[8,8,128]{2,1,0:T(8,128)S(1)} %copy.12, s32[]{:T(128)} %constant.15.clone.1), window={size=1x1x128 pad=0_0x0_0x127_0}, to_apply=%region_2.3 | reduce-window | flops 1040384 | bytes 65540 | tf_op jit(solution)/shard_map/reduce-window
  11.1 0.3 slice_reduce_fusion
  11.4 0.2 reduce-window.9
  11.6 0.1 add_bitcast_fusion
  11.7 0.8 and_reduce_fusion
  12.4 0.7 multiply_reduce_fusion.1
  13.2 8.0 %scatter_custom_fusion = s32[2048]{0:T(1024)S(1)} fusion(s32[2048]{0:T(1024)S(1)} %get-tuple-element.6, s32[2048]{0:T(1024)S(1)} %get-tuple-element.5, s32[]{:T(128)} %constant.5.clone.1), kind=kCustom, calls=%fused_computation.40 | custom fusion | bytes 8196
  21.3 1.8 concatenate.6
  23.1 9.7 %gather_fusion = bf16[2048,1024]{1,0:T(8,128)(2,1)} fusion(bf16[1025,1024]{1,0:T(8,128)(2,1)S(1)} %concatenate.6, s32[2048]{0:T(1024)S(1)} %bitcast_clamp_fusion), kind=kCustom, calls=%fused_computation | custom fusion | bytes 8396800 | tf_op jit(solution)/shard_map/gather | solution.py:36
  32.8 4.9 %convolution_convert_fusion = bf16[2,1024,256]{2,1,0:T(8,128)(2,1)} fusion(bf16[2,1024,1024]{2,1,0:T(8,128)(2,1)} %bitcast.61, bf16[2,1024,256]{2,1,0:T(8,128)(2,1)} %all-gather.3.cloned.1.call-done), kind=kOutput, calls=%fused_computation.7 | convolution fusion | flops 1074266112 | bytes 6291456 | tf_op jit(solution)/shard_map/esd,edr->esr/dot_general | solution.py:38
  37.7 0.0 reduce-scatter.2.cloned.1.call-start
  37.8 0.6 convolution_convert_fusion.1
  38.4 21.4 %psum.14 = bf16[1024,8]{0,1:T(8,128)(2,1)S(1)} all-reduce(bf16[1024,8]{0,1:T(8,128)(2,1)S(1)} %convolution_convert_fusion.1), channel_id=1, replica_groups=mesh['batch'=2,'expert'=4,'dim'=4] {'dim'}, use_global_device_ids=true, to_apply=%region_0.0 | all-reduce | flops 8192 | bytes 32768 | tf_op jit(solution)/shard_map/psum | solution.py:46
  59.9 2.0 %all_gather.10 = bf16[2,256,256]{2,1,0:T(8,128)(2,1)S(1)} all-gather(bf16[2,128,256]{2,1,0:T(8,128)(2,1)S(1)} %copy-done.2), channel_id=1, replica_groups=mesh['batch'=2,'expert'=4,'dim'=4] {'batch'}, dimensions={1}, use_global_device_ids=true | all-gather | bytes 393216 | tf_op jit(solution)/shard_map/all_gather | solution.py:44
  61.9 30.9 %all-reduce.3.cloned.1.call-done = bf16[2,1024,256]{2,1,0:T(8,128)(2,1)} async-done(((bf16[2,1024,256]{2,1,0:T(8,128)(2,1)}), bf16[2,1024,256]{2,1,0:T(8,128)(2,1)}) %all-reduce.3.cloned.1.call-update) | async-done | bytes 1048592 | tf_op jit(solution)/shard_map/psum | solution.py:47
  92.8 6.5 %fusion = f32[2,1024,1024]{2,1,0:T(8,128)} fusion(bf16[2,1024,256]{2,1,0:T(8,128)(2,1)} %all-gather.5.cloned.1.call-done, bf16[2,256,256]{2,1,0:T(8,128)(2,1)S(1)} %all_gather.10, bf16[2,1024,256]{2,1,0:T(8,128)(2,1)} %all-reduce.3.cloned.1.call-done), kind=kOutput, calls=%fused_computation.8 | convolution fusion | flops 1343750144 | bytes 10747904 | tf_op jit(solution)/shard_map/esr,edr->esd/dot_general | solution.py:54
  99.3 44.0 %gather_fusion.1 = f32[2048,1024]{1,0:T(8,128)} fusion(f32[2,1024,1024]{2,1,0:T(8,128)} %fusion, s32[2048]{0:T(1024)S(1)} %bitcast.59), kind=kCustom, calls=%fused_computation.1 | custom fusion | bytes 16793600 | tf_op jit(solution)/shard_map/vmap()/gather | solution.py:10
  143.3 4.3 %multiply_reduce_fusion = f32[1024,1024]{1,0:T(8,128)S(1)} fusion(f32[2,1024,1024]{2,1,0:T(8,128)} %bitcast.60, f32[1024]{0:T(1024)S(1)} %copy-done.3, f32[2,1024]{1,0:T(2,128)S(1)} %fusion.9), kind=kLoop, calls=%fused_computation.3 | loop fusion | flops 5242880 | bytes 12595200 | tf_op jit(solution)/shard_map/reduce_sum | solution.py:65
  147.5 2.2 %multiply_convert_fusion = bf16[1024,1024]{1,0:T(8,128)(2,1)} fusion(f32[1024,1024]{1,0:T(8,128)S(1)} %multiply_reduce_fusion, bf16[1024,1024]{1,0:T(8,128)(2,1)S(1)} %copy-done.1), kind=kLoop, calls=%fused_computation.4 | loop fusion | flops 3145728 | bytes 8388608 | tf_op jit(solution)/shard_map/convert_element_type | solution.py:68
  149.8 35.6 %reduce-scatter.2.cloned.1.call-done = bf16[256,1024]{1,0:T(8,128)(2,1)} async-done(((bf16[1024,1024]{1,0:T(8,128)(2,1)}), bf16[256,1024]{1,0:T(8,128)(2,1)}) %reduce-scatter.2.cloned.1.call-update) | async-done | bytes 524304 | tf_op jit(solution)/shard_map/reduce_scatter | solution.py:67
  185.4 2.0 %add_convert_fusion = bf16[256,1024]{1,0:T(8,128)(2,1)} fusion(bf16[256,1024]{1,0:T(8,128)(2,1)} %reduce-scatter.2.cloned.1.call-done, bf16[1024,1024]{1,0:T(8,128)(2,1)S(1)} %copy-done.1, s32[]{:T(128)S(6)} %select_n.23), kind=kLoop, calls=%fused_computation.10 | loop fusion | flops 1048576 | bytes 1572868 | tf_op jit(solution)/shard_map/convert_element_type | solution.py:72
  (28 shorter events, 0.3 us)
Async XLA Ops:
  6.5 31.2 %copy-start = (bf16[1024,8]{0,1:T(8,128)(2,1)S(1)}, bf16[1024,8]{0,1:T(8,128)(2,1)}, u32[]{:S(2)}) copy-start(bf16[1024,8]{0,1:T(8,128)(2,1)} %param.9) | copy-start | bytes 49156
  6.5 26.2 %all-gather.3.cloned.1.call-start = ((), (), s32[]{:S(2)}) async-start(), calls=%async_computation.1 | async-start | bytes 1572864 | tf_op jit(solution)/shard_map/all_gather | solution.py:41
  7.3 54.7 %all-gather.5.cloned.1.call-start = ((), (), s32[]{:S(2)}) async-start(), calls=%async_computation.3 | async-start | bytes 1572864 | tf_op jit(solution)/shard_map/all_gather | solution.py:57
  8.0 84.8 %all-reduce.3.cloned.1.call-start = ((), (), s32[]{:S(2)}) async-start(), calls=%async_computation.2 | async-start | bytes 2097152 | tf_op jit(solution)/shard_map/psum | solution.py:47
  32.8 5.0 %copy-start.1 = (bf16[1024,1024]{1,0:T(8,128)(2,1)S(1)}, bf16[1024,1024]{1,0:T(8,128)(2,1)}, u32[]{:S(2)}) copy-start(bf16[1024,1024]{1,0:T(8,128)(2,1)} %param.7) | copy-start | bytes 6291460
  32.8 27.1 %copy-start.2 = (bf16[2,128,256]{2,1,0:T(8,128)(2,1)S(1)}, bf16[2,128,256]{2,1,0:T(8,128)(2,1)}, u32[]{:S(2)}) copy-start(bf16[2,128,256]{2,1,0:T(8,128)(2,1)} %param.11) | copy-start | bytes 393220
  37.7 147.7 %reduce-scatter.2.cloned.1.call-start = ((), (), s32[]{:S(2)}) async-start(), calls=%async_computation.4 | async-start | bytes 2621440 | tf_op jit(solution)/shard_map/reduce_scatter | solution.py:67
  99.3 44.0 %copy-start.3 = (f32[1024]{0:T(1024)S(1)}, f32[1024]{0:T(1024)}, u32[]{:S(2)}) copy-start(f32[1024]{0:T(1024)} %param.13) | copy-start | bytes 12292
Sparse Core Ops, SparseCore 0:
  8.9 11.7 all-gather.2
  22.2 10.1 all-gather.4
  37.8 54.9 all-reduce.2
  149.9 35.4 reduce-scatter.1
where the time goes:
time: 195 us; the launch traced here: 194 us
  waiting for transfers between devices  68 us (35%)
  local copies, waits for them, and re-layouts  63.8 us (33%)
  blocking collectives  23.4 us (12%)
  other arithmetic  13.4 us (7%)
  between operations  13.3 us (7%)
  matrix products  12 us (6%)
    gather x1, local copies, waits for them, and re-layouts, pick_rows(): return expert_rows[slot_pick]  44 us
    reduce_scatter x1, waiting for transfers between devices, on_device(): lax.psum_scatter(partial_term.astype(jnp.bfloat16), 'expert', scatter_dim...  35.6 us
    psum x1, waiting for transfers between devices, on_device(): lax.psum(projected.astype(jnp.bfloat16), 'dim').astype(jnp.float32)  30.9 us
    psum x1, blocking collectives, on_device(): lax.psum(logits_part.astype(jnp.bfloat16), 'dim').astype(jnp.float32)  21.4 us
    gather x1, local copies, waits for them, and re-layouts, on_device(): dispatched = padded[slot_owner]  9.67 us
    unnamed x12, local copies, waits for them, and re-layouts  8.09 us
    dot_general x1, matrix products, on_device(): jnp.einsum('esr,edr->esd', hidden, lax.all_gather(expand_weight, 'batch',...  6.48 us
    dot_general x1, matrix products, on_device(): jnp.einsum('esd,edr->esr', dispatched, lax.all_gather(reduce_weight, 'bat...  4.9 us
  transfers between devices with their start and end apart: 4, of which 2 were waited for; matrix products, arithmetic and copies ran while one was open for 16% of the time, Pallas kernels for 0%

commit v1 on v0

--- a/solution.py
+++ b/solution.py
@@ -44,7 +44,7 @@
     middle_full = lax.all_gather(middle_weight, "batch", axis=1, tiled=True)
     logits, summed = (
         lax.psum(logits_part.astype(jnp.bfloat16), "dim").astype(jnp.float32),
-        lax.psum(projected.astype(jnp.bfloat16), "dim").astype(jnp.float32),
+        jnp.sum(lax.all_gather(projected.astype(jnp.bfloat16), "dim"), axis=0).astype(jnp.float32),
     )
     squashed = jnp.tanh(summed).astype(jnp.bfloat16)
     inner_mix = jnp.einsum(

time: 195 us -> 234 us (1.20)
  waiting for transfers between devices: 68 us -> 104 us
  other arithmetic: 13.4 us -> 16.5 us
    all_gather x0 -> x1, waiting for transfers between devices: none -> 59 us  [on_device(): lax.all_gather(projected.astype(jnp.bfloat16), 'dim')]
    psum x1 -> x0, waiting for transfers between devices: 30.9 us -> none  [on_device(): lax.psum(projected.astype(jnp.bfloat16), 'dim').astype(jnp.float32)]
    all_gather x1, waiting for transfers between devices: 0.02 us -> 5.93 us  [on_device(): lax.all_gather(expand_weight, 'batch', axis=1, tiled=True)]
    reduce_sum x0 -> x1, other arithmetic: none -> 3.17 us  [on_device(): jnp.sum(lax.all_gather(projected.astype(jnp.bfloat16), 'dim'), axis=0)]
  transfers between devices with their start and end apart: 4 -> 4, of which waited for: 2 -> 3; matrix products, arithmetic and copies ran while one was open for 16% -> 12% of each run, Pallas kernels for 0% -> 0%
where the time goes in v1:
time: 234 us; the launch traced here: 233 us
  waiting for transfers between devices  104 us (44%)
  local copies, waits for them, and re-layouts  63.8 us (27%)
  blocking collectives  23.3 us (10%)
  other arithmetic  16.5 us (7%)
  between operations  13.3 us (6%)
  matrix products  11.7 us (5%)
    all_gather x1, waiting for transfers between devices, on_device(): lax.all_gather(projected.astype(jnp.bfloat16), 'dim')  59 us
    gather x1, local copies, waits for them, and re-layouts, pick_rows(): return expert_rows[slot_pick]  44 us
    reduce_scatter x1, waiting for transfers between devices, on_device(): lax.psum_scatter(partial_term.astype(jnp.bfloat16), 'expert', scatter_dim...  37.5 us
    psum x1, blocking collectives, on_device(): lax.psum(logits_part.astype(jnp.bfloat16), 'dim').astype(jnp.float32)  21.3 us
    gather x1, local copies, waits for them, and re-layouts, on_device(): dispatched = padded[slot_owner]  9.67 us
    unnamed x12, local copies, waits for them, and re-layouts  8.09 us
    dot_general x1, matrix products, on_device(): jnp.einsum('esr,edr->esd', hidden, lax.all_gather(expand_weight, 'batch',...  6.18 us
    all_gather x1, waiting for transfers between devices, on_device(): lax.all_gather(expand_weight, 'batch', axis=1, tiled=True)  5.93 us
  transfers between devices with their start and end apart: 4, of which 3 were waited for; matrix products, arithmetic and copies ran while one was open for 12% of the time, Pallas kernels for 0%

profile of v1, /device:TPU:0, one launch (start us, length us, event | category | flops | bytes accessed | tf_op | source)
XLA Modules:
  0.0 232.5 jit_solution(11750584277455326027)
XLA Ops:
  6.5 0.7 all-gather.5.cloned.1.call-update
  7.3 0.7 convert_reduce_fusion
  8.1 2.3 reduce-window.6
  10.3 0.3 slice_reduce_fusion
  10.6 0.2 reduce-window.9
  10.9 0.7 multiply_reduce_fusion.1
  11.7 0.8 and_reduce_fusion
  12.5 8.0 %scatter_custom_fusion = s32[2048]{0:T(1024)S(1)} fusion(s32[2048]{0:T(1024)S(1)} %get-tuple-element.6, s32[2048]{0:T(1024)S(1)} %get-tuple-element.5, s32[]{:T(128)} %constant.6.clone.1), kind=kCustom, calls=%fused_computation.40 | custom fusion | bytes 8196
  20.5 1.8 concatenate.6
  22.3 9.7 %gather_fusion = bf16[2048,1024]{1,0:T(8,128)(2,1)} fusion(bf16[1025,1024]{1,0:T(8,128)(2,1)S(1)} %concatenate.6, s32[2048]{0:T(1024)S(1)} %bitcast_clamp_fusion), kind=kCustom, calls=%fused_computation | custom fusion | bytes 8396800 | tf_op jit(solution)/shard_map/gather | solution.py:36
  32.0 4.9 %convolution_convert_fusion = bf16[2,1024,256]{2,1,0:T(8,128)(2,1)} fusion(bf16[2,1024,1024]{2,1,0:T(8,128)(2,1)} %bitcast.62, bf16[2,1024,256]{2,1,0:T(8,128)(2,1)} %all-gather.5.cloned.1.call-done), kind=kOutput, calls=%fused_computation.7 | convolution fusion | flops 1074266112 | bytes 6291456 | tf_op jit(solution)/shard_map/esd,edr->esr/dot_general | solution.py:38
  36.9 0.7 all-gather.7.cloned.1.call-update
  37.7 0.6 convolution_convert_fusion.1
  38.4 21.3 %psum.7 = bf16[1024,8]{0,1:T(8,128)(2,1)S(1)} all-reduce(bf16[1024,8]{0,1:T(8,128)(2,1)S(1)} %convolution_convert_fusion.1), channel_id=1, replica_groups=mesh['batch'=2,'expert'=4,'dim'=4] {'dim'}, use_global_device_ids=true, to_apply=%region_0.0 | all-reduce | flops 8192 | bytes 32768 | tf_op jit(solution)/shard_map/psum | solution.py:46
  59.7 2.0 all_gather.18
  61.7 59.0 %all-gather.9.cloned.1.call-done = bf16[8,1024,256]{2,1,0:T(8,128)(2,1)} async-done(((bf16[2,1024,256]{2,1,0:T(8,128)(2,1)}), bf16[8,1024,256]{2,1,0:T(8,128)(2,1)}) %all-gather.9.cloned.1.call-update) | async-done | bytes 4194320 | tf_op jit(solution)/shard_map/all_gather | solution.py:47
  120.7 3.2 %reduce_sum.31 = bf16[2,1024,256]{2,1,0:T(8,128)(2,1)S(1)} reduce(bf16[4,2,1024,256]{3,2,1,0:T(8,128)(2,1)} %bitcast.63, bf16[]{:T(256)} %constant.10.clone.1), dimensions={0}, to_apply=%region_5.6 | reduce | flops 1572864 | bytes 5242882 | tf_op jit(solution)/shard_map/reduce_sum | solution.py:47
  123.9 5.9 %all-gather.7.cloned.1.call-done = bf16[2,1024,256]{2,1,0:T(8,128)(2,1)} async-done(((bf16[2,512,256]{2,1,0:T(8,128)(2,1)}), bf16[2,1024,256]{2,1,0:T(8,128)(2,1)}) %all-gather.7.cloned.1.call-update) | async-done | bytes 1048592 | tf_op jit(solution)/shard_map/all_gather | solution.py:57
  129.8 6.2 %fusion = f32[2,1024,1024]{2,1,0:T(8,128)} fusion(bf16[2,1024,256]{2,1,0:T(8,128)(2,1)} %all-gather.7.cloned.1.call-done, bf16[2,256,256]{2,1,0:T(8,128)(2,1)S(1)} %all_gather.18, bf16[2,1024,256]{2,1,0:T(8,128)(2,1)S(1)} %reduce_sum.31), kind=kOutput, calls=%fused_computation.8 | convolution fusion | flops 1343750144 | bytes 10747904 | tf_op jit(solution)/shard_map/esr,edr->esd/dot_general | solution.py:54
  136.0 44.0 %gather_fusion.1 = f32[2048,1024]{1,0:T(8,128)} fusion(f32[2,1024,1024]{2,1,0:T(8,128)} %fusion, s32[2048]{0:T(1024)S(1)} %bitcast.60), kind=kCustom, calls=%fused_computation.1 | custom fusion | bytes 16793600 | tf_op jit(solution)/shard_map/vmap()/gather | solution.py:10
  180.0 4.3 %multiply_reduce_fusion = f32[1024,1024]{1,0:T(8,128)S(1)} fusion(f32[2,1024,1024]{2,1,0:T(8,128)} %bitcast.61, f32[1024]{0:T(1024)S(1)} %copy-done.3, f32[2,1024]{1,0:T(2,128)S(1)} %fusion.9), kind=kLoop, calls=%fused_computation.3 | loop fusion | flops 5242880 | bytes 12595200 | tf_op jit(solution)/shard_map/reduce_sum | solution.py:65
  184.3 2.2 multiply_convert_fusion
  186.5 37.5 %reduce-scatter.2.cloned.1.call-done = bf16[256,1024]{1,0:T(8,128)(2,1)} async-done(((bf16[1024,1024]{1,0:T(8,128)(2,1)}), bf16[256,1024]{1,0:T(8,128)(2,1)}) %reduce-scatter.2.cloned.1.call-update) | async-done | bytes 524304 | tf_op jit(solution)/shard_map/reduce_scatter | solution.py:67
  224.0 2.0 add_convert_fusion
  (29 shorter events, 0.4 us)
Async XLA Ops:
  6.5 31.2 %copy-start = (bf16[1024,8]{0,1:T(8,128)(2,1)S(1)}, bf16[1024,8]{0,1:T(8,128)(2,1)}, u32[]{:S(2)}) copy-start(bf16[1024,8]{0,1:T(8,128)(2,1)} %param.9) | copy-start | bytes 49156
  6.5 25.5 %all-gather.5.cloned.1.call-start = ((), (), s32[]{:S(2)}) async-start(), calls=%async_computation.1 | async-start | bytes 1572864 | tf_op jit(solution)/shard_map/all_gather | solution.py:41
  7.3 113.5 %all-gather.9.cloned.1.call-start = ((), (), s32[]{:S(2)}) async-start(), calls=%async_computation.4 | async-start | bytes 5242880 | tf_op jit(solution)/shard_map/all_gather | solution.py:47
  32.0 5.7 %copy-start.1 = (bf16[1024,1024]{1,0:T(8,128)(2,1)S(1)}, bf16[1024,1024]{1,0:T(8,128)(2,1)}, u32[]{:S(2)}) copy-start(bf16[1024,1024]{1,0:T(8,128)(2,1)} %param.7) | copy-start | bytes 6291460
  32.0 27.7 %copy-start.2 = (bf16[2,128,256]{2,1,0:T(8,128)(2,1)S(1)}, bf16[2,128,256]{2,1,0:T(8,128)(2,1)}, u32[]{:S(2)}) copy-start(bf16[2,128,256]{2,1,0:T(8,128)(2,1)} %param.11) | copy-start | bytes 393220
  36.9 92.9 %all-gather.7.cloned.1.call-start = ((), (), s32[]{:S(2)}) async-start(), calls=%async_computation.2 | async-start | bytes 1572864 | tf_op jit(solution)/shard_map/all_gather | solution.py:57
  37.6 186.4 %reduce-scatter.2.cloned.1.call-start = ((), (), s32[]{:S(2)}) async-start(), calls=%async_computation.3 | async-start | bytes 2621440 | tf_op jit(solution)/shard_map/reduce_scatter | solution.py:67
  136.0 44.0 %copy-start.3 = (f32[1024]{0:T(1024)S(1)}, f32[1024]{0:T(1024)}, u32[]{:S(2)}) copy-start(f32[1024]{0:T(1024)} %param.13) | copy-start | bytes 12292
Sparse Core Ops, SparseCore 0:
  8.9 11.7 all-gather.4
  37.0 83.6 all-gather.8
  122.3 7.5 all-gather.6
  186.6 37.3 reduce-scatter.1
